TPU v7x, 128 devices: a whole 4x4x4 slice. The times are simulated.
128 devices in a mesh: dp: 1, cpo: 16 (over z, y), cpi: 8 (over x, core).
Axes of the slice: x: 4, y: 4, z: 4, core: 2. Of those that a mesh axis runs over, the one named last changes fastest.
Arguments:
- hidden: bfloat16 [16384, 2048], P(('dp', 'cpo', 'cpi'))
- w_q: bfloat16 [2048, 16, 128], replicated
- w_k: bfloat16 [2048, 2, 128], replicated
- w_v: bfloat16 [2048, 2, 128], replicated
- w_o: bfloat16 [16, 128, 2048], replicated
Outputs:
- output: bfloat16 [16384, 2048], P(('dp', 'cpo', 'cpi'))
All inputs are finite; a program needn't handle non-finite values.
Results may differ from a plain program's by a relative error of at most 0.00605925.
Values are sent between devices in bfloat16 or wider.
A program may use at most 1 GiB of HBM per device.

v0:
```python
import jax
import jax.numpy as jnp
from jax import lax
from jax.sharding import PartitionSpec as P

WINDOW = 2048
ROPE_BASE = 10000.0


def rope_rotate(vals, positions):
    half_dim = vals.shape[-1] // 2
    inv_freq = ROPE_BASE ** (-jnp.arange(half_dim, dtype=jnp.float32) * 2.0 / vals.shape[-1])
    angles = positions.astype(jnp.float32)[..., None] * inv_freq
    cos_t = jnp.cos(angles)[..., None, :]
    sin_t = jnp.sin(angles)[..., None, :]
    lower_half = vals[..., :half_dim]
    upper_half = vals[..., half_dim:]
    return jnp.concatenate([lower_half * cos_t - upper_half * sin_t, upper_half * cos_t + lower_half * sin_t], axis=-1)


def project_local(hidden, w_q, w_k, w_v, positions):
    q_rot = rope_rotate(jnp.einsum('td,dhe->the', hidden, w_q, preferred_element_type=jnp.float32), positions).astype(jnp.bfloat16)
    k_rot = rope_rotate(jnp.einsum('td,dhe->the', hidden, w_k, preferred_element_type=jnp.float32), positions).astype(jnp.bfloat16)
    v_val = jnp.einsum('td,dhe->the', hidden, w_v, preferred_element_type=jnp.float32).astype(jnp.bfloat16)
    return q_rot, k_rot, v_val


def attend_step(soft_state, q_grp, k_blk, v_blk, back_step, source_ok):
    run_max, run_sum, run_acc = soft_state
    tok_count = q_grp.shape[0]
    score_scale = q_grp.shape[-1] ** -0.5
    scores = jnp.einsum('tkgd,skd->kgts', q_grp, k_blk, preferred_element_type=jnp.float32) * score_scale
    tok_idx = jnp.arange(tok_count)
    pos_gap = back_step * tok_count + tok_idx[:, None] - tok_idx[None, :]
    allowed = (pos_gap >= 0) & (pos_gap < WINDOW) & source_ok
    scores = jnp.where(allowed, scores, -jnp.inf)
    new_max = jnp.maximum(run_max, jnp.max(scores, axis=-1))
    exp_scores = jnp.exp(scores - new_max[..., None])
    rescale = jnp.exp(run_max - new_max)
    run_sum = run_sum * rescale + jnp.sum(exp_scores, axis=-1)
    run_acc = run_acc * rescale[..., None] + jnp.einsum('kgts,skd->kgtd', exp_scores.astype(jnp.bfloat16), v_blk, preferred_element_type=jnp.float32)
    return new_max, run_sum, run_acc


def finish_output(soft_state, w_o):
    run_max, run_sum, run_acc = soft_state
    heads_kv, group_size = run_acc.shape[0], run_acc.shape[1]
    attended = (run_acc / run_sum[..., None]).astype(jnp.bfloat16)
    w_grp = w_o.reshape(heads_kv, group_size, w_o.shape[1], w_o.shape[2])
    return jnp.einsum('kgtd,kgde->te', attended, w_grp, preferred_element_type=jnp.float32).astype(jnp.bfloat16)


def solution(mesh):
    n_outer = mesh.shape['cpo']
    n_inner = mesh.shape['cpi']
    n_shards = n_outer * n_inner
    shift_perm = [(source, source + 1) for source in range(n_shards - 1)]

    def local_fn(hidden, w_q, w_k, w_v, w_o):
        tok_count = hidden.shape[0]
        heads_q, head_dim = w_q.shape[1], w_q.shape[2]
        heads_kv = w_k.shape[1]
        group_size = heads_q // heads_kv
        n_back = min((WINDOW + tok_count - 2) // tok_count, n_shards - 1)
        shard_rank = lax.axis_index('cpo') * n_inner + lax.axis_index('cpi')
        positions = shard_rank * tok_count + jnp.arange(tok_count)
        q_rot, k_cur, v_cur = project_local(hidden, w_q, w_k, w_v, positions)
        q_grp = q_rot.reshape(tok_count, heads_kv, group_size, head_dim)
        soft_state = (jnp.full((heads_kv, group_size, tok_count), -jnp.inf, jnp.float32),
                      jnp.zeros((heads_kv, group_size, tok_count), jnp.float32),
                      jnp.zeros((heads_kv, group_size, tok_count, head_dim), jnp.float32))
        soft_state = attend_step(soft_state, q_grp, k_cur, v_cur, 0, True)
        for back_step in range(1, n_back + 1):
            k_cur = lax.ppermute(k_cur, ('cpo', 'cpi'), shift_perm)
            v_cur = lax.ppermute(v_cur, ('cpo', 'cpi'), shift_perm)
            soft_state = attend_step(soft_state, q_grp, k_cur, v_cur, back_step, shard_rank >= back_step)
        return finish_output(soft_state, w_o)

    return jax.shard_map(local_fn, mesh=mesh,
                         in_specs=(P(('dp', 'cpo', 'cpi'), None), P(), P(), P(), P()),
                         out_specs=P(('dp', 'cpo', 'cpi'), None), check_vma=False)
```

profile of v0, /device:TPU:96, one launch (start us, length us, event | category | flops | bytes accessed | tf_op | source)
XLA Modules:
  0.0 196.5 jit_solution(16137052103327689813)
XLA Ops:
  0.0 2.5 %copy.6 = bf16[2048,2,128]{0,2,1:T(8,128)(2,1)S(1)} copy(bf16[2048,2,128]{2,1,0:T(2,128)(2,1)} %param.7) | data formatting | bytes 2097152 | tf_op args[2]
  4.3 1.9 collective-permute-start
  7.6 3.5 %collective-permute-start.1 = (bf16[128,2,128]{2,0,1:T(8,128)(2,1)S(1)}, bf16[128,2,128]{2,0,1:T(8,128)(2,1)S(1)}, u32[]{:S(2)}, u32[]{:S(2)}) collective-permute-start(bf16[128,2,128]{2,0,1:T(8,128)(2,1)S(1)} %convolution_convert_fusion), channel_id=1, source_target_pairs={{0,1},{1,2},{2,3},{3,4},{4,5},{5,6},{6,7},{7,8},{8,9},{9,10},{10,1... | collective-permute-start | bytes 196616 | tf_op jit(solution)/shard_map/ppermute | solution.py:75
  11.3 12.4 %copy.7 = bf16[2048,16,128]{0,2,1:T(8,128)(2,1)} copy(bf16[2048,16,128]{2,1,0:T(8,128)(2,1)} %param.6) | data formatting | bytes 16777216 | tf_op args[1]
  23.7 5.8 %fusion.236 = f32[128,2048]{0,1:S(1)} fusion(bf16[128,2048]{1,0:T(8,128)(2,1)S(1)} %copy-done.2, bf16[2048,2048]{0,1:T(8,128)(2,1)} %bitcast.276), kind=kOutput, calls=%fused_computation.343 | convolution fusion | flops 1073741824 | bytes 9961472
  31.6 1.9 collective-permute-start.2
  33.9 3.5 %collective-permute-start.3 = (bf16[128,2,128]{2,0,1:T(8,128)(2,1)S(1)}, bf16[128,2,128]{2,0,1:T(8,128)(2,1)S(1)}, u32[]{:S(2)}, u32[]{:S(2)}) collective-permute-start(bf16[128,2,128]{2,0,1:T(8,128)(2,1)S(1)} %collective-permute-done.1), channel_id=1, source_target_pairs={{0,1},{1,2},{2,3},{3,4},{4,5},{5,6},{6,7},{7,8},{8,9},{9,10},{10,1... | collective-permute-start | bytes 196616 | tf_op jit(solution)/shard_map/ppermute | solution.py:75
  37.4 4.0 %collective-permute-done.2 = bf16[128,2,128]{0,2,1:T(8,128)(2,1)S(1)} collective-permute-done((bf16[128,2,128]{0,2,1:T(8,128)(2,1)S(1)}, bf16[128,2,128]{0,2,1:T(8,128)(2,1)S(1)}, u32[]{:S(2)}, u32[]{:S(2)}) %collective-permute-start.2) | collective-permute-done | bytes 65568 | tf_op jit(solution)/shard_map/ppermute | solution.py:74
  41.4 1.9 collective-permute-start.4
  45.6 5.6 %collective-permute-done.4 = bf16[128,2,128]{0,2,1:T(8,128)(2,1)S(1)} collective-permute-done((bf16[128,2,128]{0,2,1:T(8,128)(2,1)S(1)}, bf16[128,2,128]{0,2,1:T(8,128)(2,1)S(1)}, u32[]{:S(2)}, u32[]{:S(2)}) %collective-permute-start.4) | collective-permute-done | bytes 65568 | tf_op jit(solution)/shard_map/ppermute | solution.py:74
  53.5 1.9 collective-permute-start.7
  55.4 5.6 %collective-permute-done.6 = bf16[128,2,128]{0,2,1:T(8,128)(2,1)S(1)} collective-permute-done((bf16[128,2,128]{0,2,1:T(8,128)(2,1)S(1)}, bf16[128,2,128]{0,2,1:T(8,128)(2,1)S(1)}, u32[]{:S(2)}, u32[]{:S(2)}) %collective-permute-start.6) | collective-permute-done | bytes 65568 | tf_op jit(solution)/shard_map/ppermute | solution.py:74
  61.0 1.9 collective-permute-start.8
  65.2 5.6 %collective-permute-done.8 = bf16[128,2,128]{0,2,1:T(8,128)(2,1)S(1)} collective-permute-done((bf16[128,2,128]{0,2,1:T(8,128)(2,1)S(1)}, bf16[128,2,128]{0,2,1:T(8,128)(2,1)S(1)}, u32[]{:S(2)}, u32[]{:S(2)}) %collective-permute-start.8) | collective-permute-done | bytes 65568 | tf_op jit(solution)/shard_map/ppermute | solution.py:74
  75.0 5.6 %collective-permute-done.10 = bf16[128,2,128]{0,2,1:T(8,128)(2,1)S(1)} collective-permute-done((bf16[128,2,128]{0,2,1:T(8,128)(2,1)S(1)}, bf16[128,2,128]{0,2,1:T(8,128)(2,1)S(1)}, u32[]{:S(2)}, u32[]{:S(2)}) %collective-permute-start.10) | collective-permute-done | bytes 65568 | tf_op jit(solution)/shard_map/ppermute | solution.py:74
  80.6 1.9 collective-permute-start.12
  82.9 1.9 collective-permute-start.13
  84.8 5.6 %collective-permute-done.12 = bf16[128,2,128]{0,2,1:T(8,128)(2,1)S(1)} collective-permute-done((bf16[128,2,128]{0,2,1:T(8,128)(2,1)S(1)}, bf16[128,2,128]{0,2,1:T(8,128)(2,1)S(1)}, u32[]{:S(2)}, u32[]{:S(2)}) %collective-permute-start.12) | collective-permute-done | bytes 65568 | tf_op jit(solution)/shard_map/ppermute | solution.py:74
  94.6 5.6 %collective-permute-done.14 = bf16[128,2,128]{0,2,1:T(8,128)(2,1)S(1)} collective-permute-done((bf16[128,2,128]{0,2,1:T(8,128)(2,1)S(1)}, bf16[128,2,128]{0,2,1:T(8,128)(2,1)S(1)}, u32[]{:S(2)}, u32[]{:S(2)}) %collective-permute-start.14) | collective-permute-done | bytes 65568 | tf_op jit(solution)/shard_map/ppermute | solution.py:74
  102.5 1.9 collective-permute-start.17
  104.4 5.6 %collective-permute-done.16 = bf16[128,2,128]{0,2,1:T(8,128)(2,1)S(1)} collective-permute-done((bf16[128,2,128]{0,2,1:T(8,128)(2,1)S(1)}, bf16[128,2,128]{0,2,1:T(8,128)(2,1)S(1)}, u32[]{:S(2)}, u32[]{:S(2)}) %collective-permute-start.16) | collective-permute-done | bytes 65568 | tf_op jit(solution)/shard_map/ppermute | solution.py:74
  110.0 1.9 collective-permute-start.18
  114.2 5.6 %collective-permute-done.18 = bf16[128,2,128]{0,2,1:T(8,128)(2,1)S(1)} collective-permute-done((bf16[128,2,128]{0,2,1:T(8,128)(2,1)S(1)}, bf16[128,2,128]{0,2,1:T(8,128)(2,1)S(1)}, u32[]{:S(2)}, u32[]{:S(2)}) %collective-permute-start.18) | collective-permute-done | bytes 65568 | tf_op jit(solution)/shard_map/ppermute | solution.py:74
  124.0 5.6 %collective-permute-done.20 = bf16[128,2,128]{0,2,1:T(8,128)(2,1)S(1)} collective-permute-done((bf16[128,2,128]{0,2,1:T(8,128)(2,1)S(1)}, bf16[128,2,128]{0,2,1:T(8,128)(2,1)S(1)}, u32[]{:S(2)}, u32[]{:S(2)}) %collective-permute-start.20) | collective-permute-done | bytes 65568 | tf_op jit(solution)/shard_map/ppermute | solution.py:74
  133.8 5.6 %collective-permute-done.22 = bf16[128,2,128]{0,2,1:T(8,128)(2,1)S(1)} collective-permute-done((bf16[128,2,128]{0,2,1:T(8,128)(2,1)S(1)}, bf16[128,2,128]{0,2,1:T(8,128)(2,1)S(1)}, u32[]{:S(2)}, u32[]{:S(2)}) %collective-permute-start.22) | collective-permute-done | bytes 65568 | tf_op jit(solution)/shard_map/ppermute | solution.py:74
  143.6 5.6 %collective-permute-done.24 = bf16[128,2,128]{0,2,1:T(8,128)(2,1)S(1)} collective-permute-done((bf16[128,2,128]{0,2,1:T(8,128)(2,1)S(1)}, bf16[128,2,128]{0,2,1:T(8,128)(2,1)S(1)}, u32[]{:S(2)}, u32[]{:S(2)}) %collective-permute-start.24) | collective-permute-done | bytes 65568 | tf_op jit(solution)/shard_map/ppermute | solution.py:74
  153.4 5.6 %collective-permute-done.26 = bf16[128,2,128]{0,2,1:T(8,128)(2,1)S(1)} collective-permute-done((bf16[128,2,128]{0,2,1:T(8,128)(2,1)S(1)}, bf16[128,2,128]{0,2,1:T(8,128)(2,1)S(1)}, u32[]{:S(2)}, u32[]{:S(2)}) %collective-permute-start.26) | collective-permute-done | bytes 65568 | tf_op jit(solution)/shard_map/ppermute | solution.py:74
  158.9 2.1 %collective-permute-start.28 = (bf16[128,2,128]{0,2,1:T(8,128)(2,1)S(1)}, bf16[128,2,128]{0,2,1:T(8,128)(2,1)S(1)}, u32[]{:S(2)}, u32[]{:S(2)}) collective-permute-start(bf16[128,2,128]{0,2,1:T(8,128)(2,1)S(1)} %collective-permute-done.26), channel_id=1, source_target_pairs={{0,1},{1,2},{2,3},{3,4},{4,5},{5,6},{6,7},{7,8},{8,9},{9,10},{10,1... | collective-permute-start | bytes 196616 | tf_op jit(solution)/shard_map/ppermute | solution.py:74
  161.4 1.9 collective-permute-start.29
  163.3 5.4 %collective-permute-done.28 = bf16[128,2,128]{0,2,1:T(8,128)(2,1)S(1)} collective-permute-done((bf16[128,2,128]{0,2,1:T(8,128)(2,1)S(1)}, bf16[128,2,128]{0,2,1:T(8,128)(2,1)S(1)}, u32[]{:S(2)}, u32[]{:S(2)}) %collective-permute-start.28) | collective-permute-done | bytes 65568 | tf_op jit(solution)/shard_map/ppermute | solution.py:74
  173.1 5.4 %collective-permute-done.30 = bf16[128,2,128]{0,2,1:T(8,128)(2,1)S(1)} collective-permute-done((bf16[128,2,128]{0,2,1:T(8,128)(2,1)S(1)}, bf16[128,2,128]{0,2,1:T(8,128)(2,1)S(1)}, u32[]{:S(2)}, u32[]{:S(2)}) %collective-permute-start.30) | collective-permute-done | bytes 65568 | tf_op jit(solution)/shard_map/ppermute | solution.py:74
  190.9 5.7 %fusion.5 = bf16[128,2048]{1,0:T(8,128)(2,1)} fusion(bf16[2,8,128,2048]{3,2,1,0:T(8,128)(2,1)} %bitcast.282, f32[2,8,128,128]{3,2,0,1:T(8,128)S(1)} %fusion.11, bf16[2,8,128,128]{2,3,1,0:T(8,128)(2,1)S(1)} %get-tuple-element.40, f32[2,8,128]{2,0,1:T(2,128)S(1)} %copy.45, bf16[128,2,128]{2,0,1:T(8,128)(2,1)S(1)} %collective-permute-done.31), kind=kOutput, calls=%fused_computation.3 | convolution fusion | flops 1141899264 | bytes 10559488 | tf_op jit(solution)/shard_map/kgtd,kgde->te/dot_general | solution.py:50
  (156 shorter events, 59.3 us)
Async XLA Ops:
  4.3 27.3 %collective-permute-start = (bf16[128,2,128]{0,2,1:T(8,128)(2,1)S(1)}, bf16[128,2,128]{0,2,1:T(8,128)(2,1)S(1)}, u32[]{:S(2)}, u32[]{:S(2)}) collective-permute-start(bf16[128,2,128]{0,2,1:T(8,128)(2,1)S(1)} %pad_maximum_fusion.1), channel_id=1, source_target_pairs={{0,1},{1,2},{2,3},{3,4},{4,5},{5,6},{6,7},{7,8},{8,9},{9,10},{10,1... | collective-permute-start | bytes 196616 | tf_op jit(solution)/shard_map/ppermute | solution.py:74
  7.6 26.3 %collective-permute-start.1 = (bf16[128,2,128]{2,0,1:T(8,128)(2,1)S(1)}, bf16[128,2,128]{2,0,1:T(8,128)(2,1)S(1)}, u32[]{:S(2)}, u32[]{:S(2)}) collective-permute-start(bf16[128,2,128]{2,0,1:T(8,128)(2,1)S(1)} %convolution_convert_fusion), channel_id=1, source_target_pairs={{0,1},{1,2},{2,3},{3,4},{4,5},{5,6},{6,7},{7,8},{8,9},{9,10},{10,1... | collective-permute-start | bytes 196616 | tf_op jit(solution)/shard_map/ppermute | solution.py:75
  31.6 9.8 %collective-permute-start.2 = (bf16[128,2,128]{0,2,1:T(8,128)(2,1)S(1)}, bf16[128,2,128]{0,2,1:T(8,128)(2,1)S(1)}, u32[]{:S(2)}, u32[]{:S(2)}) collective-permute-start(bf16[128,2,128]{0,2,1:T(8,128)(2,1)S(1)} %collective-permute-done), channel_id=1, source_target_pairs={{0,1},{1,2},{2,3},{3,4},{4,5},{5,6},{6,7},{7,8},{8,9},{9,10},{10,1... | collective-permute-start | bytes 196616 | tf_op jit(solution)/shard_map/ppermute | solution.py:74
  33.9 9.8 %collective-permute-start.3 = (bf16[128,2,128]{2,0,1:T(8,128)(2,1)S(1)}, bf16[128,2,128]{2,0,1:T(8,128)(2,1)S(1)}, u32[]{:S(2)}, u32[]{:S(2)}) collective-permute-start(bf16[128,2,128]{2,0,1:T(8,128)(2,1)S(1)} %collective-permute-done.1), channel_id=1, source_target_pairs={{0,1},{1,2},{2,3},{3,4},{4,5},{5,6},{6,7},{7,8},{8,9},{9,10},{10,1... | collective-permute-start | bytes 196616 | tf_op jit(solution)/shard_map/ppermute | solution.py:75
  41.4 9.8 %collective-permute-start.4 = (bf16[128,2,128]{0,2,1:T(8,128)(2,1)S(1)}, bf16[128,2,128]{0,2,1:T(8,128)(2,1)S(1)}, u32[]{:S(2)}, u32[]{:S(2)}) collective-permute-start(bf16[128,2,128]{0,2,1:T(8,128)(2,1)S(1)} %collective-permute-done.2), channel_id=1, source_target_pairs={{0,1},{1,2},{2,3},{3,4},{4,5},{5,6},{6,7},{7,8},{8,9},{9,10},{10,1... | collective-permute-start | bytes 196616 | tf_op jit(solution)/shard_map/ppermute | solution.py:74
  43.7 9.8 %collective-permute-start.5 = (bf16[128,2,128]{2,0,1:T(8,128)(2,1)S(1)}, bf16[128,2,128]{2,0,1:T(8,128)(2,1)S(1)}, u32[]{:S(2)}, u32[]{:S(2)}) collective-permute-start(bf16[128,2,128]{2,0,1:T(8,128)(2,1)S(1)} %collective-permute-done.3), channel_id=1, source_target_pairs={{0,1},{1,2},{2,3},{3,4},{4,5},{5,6},{6,7},{7,8},{8,9},{9,10},{10,1... | collective-permute-start | bytes 196616 | tf_op jit(solution)/shard_map/ppermute | solution.py:75
  51.2 9.8 %collective-permute-start.6 = (bf16[128,2,128]{0,2,1:T(8,128)(2,1)S(1)}, bf16[128,2,128]{0,2,1:T(8,128)(2,1)S(1)}, u32[]{:S(2)}, u32[]{:S(2)}) collective-permute-start(bf16[128,2,128]{0,2,1:T(8,128)(2,1)S(1)} %collective-permute-done.4), channel_id=1, source_target_pairs={{0,1},{1,2},{2,3},{3,4},{4,5},{5,6},{6,7},{7,8},{8,9},{9,10},{10,1... | collective-permute-start | bytes 196616 | tf_op jit(solution)/shard_map/ppermute | solution.py:74
  53.5 9.8 %collective-permute-start.7 = (bf16[128,2,128]{2,0,1:T(8,128)(2,1)S(1)}, bf16[128,2,128]{2,0,1:T(8,128)(2,1)S(1)}, u32[]{:S(2)}, u32[]{:S(2)}) collective-permute-start(bf16[128,2,128]{2,0,1:T(8,128)(2,1)S(1)} %collective-permute-done.5), channel_id=1, source_target_pairs={{0,1},{1,2},{2,3},{3,4},{4,5},{5,6},{6,7},{7,8},{8,9},{9,10},{10,1... | collective-permute-start | bytes 196616 | tf_op jit(solution)/shard_map/ppermute | solution.py:75
  61.0 9.8 %collective-permute-start.8 = (bf16[128,2,128]{0,2,1:T(8,128)(2,1)S(1)}, bf16[128,2,128]{0,2,1:T(8,128)(2,1)S(1)}, u32[]{:S(2)}, u32[]{:S(2)}) collective-permute-start(bf16[128,2,128]{0,2,1:T(8,128)(2,1)S(1)} %collective-permute-done.6), channel_id=1, source_target_pairs={{0,1},{1,2},{2,3},{3,4},{4,5},{5,6},{6,7},{7,8},{8,9},{9,10},{10,1... | collective-permute-start | bytes 196616 | tf_op jit(solution)/shard_map/ppermute | solution.py:74
  63.3 9.8 %collective-permute-start.9 = (bf16[128,2,128]{2,0,1:T(8,128)(2,1)S(1)}, bf16[128,2,128]{2,0,1:T(8,128)(2,1)S(1)}, u32[]{:S(2)}, u32[]{:S(2)}) collective-permute-start(bf16[128,2,128]{2,0,1:T(8,128)(2,1)S(1)} %collective-permute-done.7), channel_id=1, source_target_pairs={{0,1},{1,2},{2,3},{3,4},{4,5},{5,6},{6,7},{7,8},{8,9},{9,10},{10,1... | collective-permute-start | bytes 196616 | tf_op jit(solution)/shard_map/ppermute | solution.py:75
  70.8 9.8 %collective-permute-start.10 = (bf16[128,2,128]{0,2,1:T(8,128)(2,1)S(1)}, bf16[128,2,128]{0,2,1:T(8,128)(2,1)S(1)}, u32[]{:S(2)}, u32[]{:S(2)}) collective-permute-start(bf16[128,2,128]{0,2,1:T(8,128)(2,1)S(1)} %collective-permute-done.8), channel_id=1, source_target_pairs={{0,1},{1,2},{2,3},{3,4},{4,5},{5,6},{6,7},{7,8},{8,9},{9,10},{10,1... | collective-permute-start | bytes 196616 | tf_op jit(solution)/shard_map/ppermute | solution.py:74
  73.1 9.8 %collective-permute-start.11 = (bf16[128,2,128]{2,0,1:T(8,128)(2,1)S(1)}, bf16[128,2,128]{2,0,1:T(8,128)(2,1)S(1)}, u32[]{:S(2)}, u32[]{:S(2)}) collective-permute-start(bf16[128,2,128]{2,0,1:T(8,128)(2,1)S(1)} %collective-permute-done.9), channel_id=1, source_target_pairs={{0,1},{1,2},{2,3},{3,4},{4,5},{5,6},{6,7},{7,8},{8,9},{9,10},{10,1... | collective-permute-start | bytes 196616 | tf_op jit(solution)/shard_map/ppermute | solution.py:75
  80.6 9.8 %collective-permute-start.12 = (bf16[128,2,128]{0,2,1:T(8,128)(2,1)S(1)}, bf16[128,2,128]{0,2,1:T(8,128)(2,1)S(1)}, u32[]{:S(2)}, u32[]{:S(2)}) collective-permute-start(bf16[128,2,128]{0,2,1:T(8,128)(2,1)S(1)} %collective-permute-done.10), channel_id=1, source_target_pairs={{0,1},{1,2},{2,3},{3,4},{4,5},{5,6},{6,7},{7,8},{8,9},{9,10},{10,1... | collective-permute-start | bytes 196616 | tf_op jit(solution)/shard_map/ppermute | solution.py:74
  82.9 9.8 %collective-permute-start.13 = (bf16[128,2,128]{2,0,1:T(8,128)(2,1)S(1)}, bf16[128,2,128]{2,0,1:T(8,128)(2,1)S(1)}, u32[]{:S(2)}, u32[]{:S(2)}) collective-permute-start(bf16[128,2,128]{2,0,1:T(8,128)(2,1)S(1)} %collective-permute-done.11), channel_id=1, source_target_pairs={{0,1},{1,2},{2,3},{3,4},{4,5},{5,6},{6,7},{7,8},{8,9},{9,10},{10,1... | collective-permute-start | bytes 196616 | tf_op jit(solution)/shard_map/ppermute | solution.py:75
  90.4 9.8 %collective-permute-start.14 = (bf16[128,2,128]{0,2,1:T(8,128)(2,1)S(1)}, bf16[128,2,128]{0,2,1:T(8,128)(2,1)S(1)}, u32[]{:S(2)}, u32[]{:S(2)}) collective-permute-start(bf16[128,2,128]{0,2,1:T(8,128)(2,1)S(1)} %collective-permute-done.12), channel_id=1, source_target_pairs={{0,1},{1,2},{2,3},{3,4},{4,5},{5,6},{6,7},{7,8},{8,9},{9,10},{10,1... | collective-permute-start | bytes 196616 | tf_op jit(solution)/shard_map/ppermute | solution.py:74
  92.7 9.8 %collective-permute-start.15 = (bf16[128,2,128]{2,0,1:T(8,128)(2,1)S(1)}, bf16[128,2,128]{2,0,1:T(8,128)(2,1)S(1)}, u32[]{:S(2)}, u32[]{:S(2)}) collective-permute-start(bf16[128,2,128]{2,0,1:T(8,128)(2,1)S(1)} %collective-permute-done.13), channel_id=1, source_target_pairs={{0,1},{1,2},{2,3},{3,4},{4,5},{5,6},{6,7},{7,8},{8,9},{9,10},{10,1... | collective-permute-start | bytes 196616 | tf_op jit(solution)/shard_map/ppermute | solution.py:75
  100.2 9.8 %collective-permute-start.16 = (bf16[128,2,128]{0,2,1:T(8,128)(2,1)S(1)}, bf16[128,2,128]{0,2,1:T(8,128)(2,1)S(1)}, u32[]{:S(2)}, u32[]{:S(2)}) collective-permute-start(bf16[128,2,128]{0,2,1:T(8,128)(2,1)S(1)} %collective-permute-done.14), channel_id=1, source_target_pairs={{0,1},{1,2},{2,3},{3,4},{4,5},{5,6},{6,7},{7,8},{8,9},{9,10},{10,1... | collective-permute-start | bytes 196616 | tf_op jit(solution)/shard_map/ppermute | solution.py:74
  102.5 9.8 %collective-permute-start.17 = (bf16[128,2,128]{2,0,1:T(8,128)(2,1)S(1)}, bf16[128,2,128]{2,0,1:T(8,128)(2,1)S(1)}, u32[]{:S(2)}, u32[]{:S(2)}) collective-permute-start(bf16[128,2,128]{2,0,1:T(8,128)(2,1)S(1)} %collective-permute-done.15), channel_id=1, source_target_pairs={{0,1},{1,2},{2,3},{3,4},{4,5},{5,6},{6,7},{7,8},{8,9},{9,10},{10,1... | collective-permute-start | bytes 196616 | tf_op jit(solution)/shard_map/ppermute | solution.py:75
  110.0 9.8 %collective-permute-start.18 = (bf16[128,2,128]{0,2,1:T(8,128)(2,1)S(1)}, bf16[128,2,128]{0,2,1:T(8,128)(2,1)S(1)}, u32[]{:S(2)}, u32[]{:S(2)}) collective-permute-start(bf16[128,2,128]{0,2,1:T(8,128)(2,1)S(1)} %collective-permute-done.16), channel_id=1, source_target_pairs={{0,1},{1,2},{2,3},{3,4},{4,5},{5,6},{6,7},{7,8},{8,9},{9,10},{10,1... | collective-permute-start | bytes 196616 | tf_op jit(solution)/shard_map/ppermute | solution.py:74
  112.3 9.8 %collective-permute-start.19 = (bf16[128,2,128]{2,0,1:T(8,128)(2,1)S(1)}, bf16[128,2,128]{2,0,1:T(8,128)(2,1)S(1)}, u32[]{:S(2)}, u32[]{:S(2)}) collective-permute-start(bf16[128,2,128]{2,0,1:T(8,128)(2,1)S(1)} %collective-permute-done.17), channel_id=1, source_target_pairs={{0,1},{1,2},{2,3},{3,4},{4,5},{5,6},{6,7},{7,8},{8,9},{9,10},{10,1... | collective-permute-start | bytes 196616 | tf_op jit(solution)/shard_map/ppermute | solution.py:75
  119.8 9.8 %collective-permute-start.20 = (bf16[128,2,128]{0,2,1:T(8,128)(2,1)S(1)}, bf16[128,2,128]{0,2,1:T(8,128)(2,1)S(1)}, u32[]{:S(2)}, u32[]{:S(2)}) collective-permute-start(bf16[128,2,128]{0,2,1:T(8,128)(2,1)S(1)} %collective-permute-done.18), channel_id=1, source_target_pairs={{0,1},{1,2},{2,3},{3,4},{4,5},{5,6},{6,7},{7,8},{8,9},{9,10},{10,1... | collective-permute-start | bytes 196616 | tf_op jit(solution)/shard_map/ppermute | solution.py:74
  122.1 9.8 %collective-permute-start.21 = (bf16[128,2,128]{2,0,1:T(8,128)(2,1)S(1)}, bf16[128,2,128]{2,0,1:T(8,128)(2,1)S(1)}, u32[]{:S(2)}, u32[]{:S(2)}) collective-permute-start(bf16[128,2,128]{2,0,1:T(8,128)(2,1)S(1)} %collective-permute-done.19), channel_id=1, source_target_pairs={{0,1},{1,2},{2,3},{3,4},{4,5},{5,6},{6,7},{7,8},{8,9},{9,10},{10,1... | collective-permute-start | bytes 196616 | tf_op jit(solution)/shard_map/ppermute | solution.py:75
  129.6 9.8 %collective-permute-start.22 = (bf16[128,2,128]{0,2,1:T(8,128)(2,1)S(1)}, bf16[128,2,128]{0,2,1:T(8,128)(2,1)S(1)}, u32[]{:S(2)}, u32[]{:S(2)}) collective-permute-start(bf16[128,2,128]{0,2,1:T(8,128)(2,1)S(1)} %collective-permute-done.20), channel_id=1, source_target_pairs={{0,1},{1,2},{2,3},{3,4},{4,5},{5,6},{6,7},{7,8},{8,9},{9,10},{10,1... | collective-permute-start | bytes 196616 | tf_op jit(solution)/shard_map/ppermute | solution.py:74
  131.9 9.8 %collective-permute-start.23 = (bf16[128,2,128]{2,0,1:T(8,128)(2,1)S(1)}, bf16[128,2,128]{2,0,1:T(8,128)(2,1)S(1)}, u32[]{:S(2)}, u32[]{:S(2)}) collective-permute-start(bf16[128,2,128]{2,0,1:T(8,128)(2,1)S(1)} %collective-permute-done.21), channel_id=1, source_target_pairs={{0,1},{1,2},{2,3},{3,4},{4,5},{5,6},{6,7},{7,8},{8,9},{9,10},{10,1... | collective-permute-start | bytes 196616 | tf_op jit(solution)/shard_map/ppermute | solution.py:75
  139.3 9.8 %collective-permute-start.24 = (bf16[128,2,128]{0,2,1:T(8,128)(2,1)S(1)}, bf16[128,2,128]{0,2,1:T(8,128)(2,1)S(1)}, u32[]{:S(2)}, u32[]{:S(2)}) collective-permute-start(bf16[128,2,128]{0,2,1:T(8,128)(2,1)S(1)} %collective-permute-done.22), channel_id=1, source_target_pairs={{0,1},{1,2},{2,3},{3,4},{4,5},{5,6},{6,7},{7,8},{8,9},{9,10},{10,1... | collective-permute-start | bytes 196616 | tf_op jit(solution)/shard_map/ppermute | solution.py:74
  141.7 9.8 %collective-permute-start.25 = (bf16[128,2,128]{2,0,1:T(8,128)(2,1)S(1)}, bf16[128,2,128]{2,0,1:T(8,128)(2,1)S(1)}, u32[]{:S(2)}, u32[]{:S(2)}) collective-permute-start(bf16[128,2,128]{2,0,1:T(8,128)(2,1)S(1)} %collective-permute-done.23), channel_id=1, source_target_pairs={{0,1},{1,2},{2,3},{3,4},{4,5},{5,6},{6,7},{7,8},{8,9},{9,10},{10,1... | collective-permute-start | bytes 196616 | tf_op jit(solution)/shard_map/ppermute | solution.py:75
  149.1 9.8 %collective-permute-start.26 = (bf16[128,2,128]{0,2,1:T(8,128)(2,1)S(1)}, bf16[128,2,128]{0,2,1:T(8,128)(2,1)S(1)}, u32[]{:S(2)}, u32[]{:S(2)}) collective-permute-start(bf16[128,2,128]{0,2,1:T(8,128)(2,1)S(1)} %collective-permute-done.24), channel_id=1, source_target_pairs={{0,1},{1,2},{2,3},{3,4},{4,5},{5,6},{6,7},{7,8},{8,9},{9,10},{10,1... | collective-permute-start | bytes 196616 | tf_op jit(solution)/shard_map/ppermute | solution.py:74
  151.5 9.9 %collective-permute-start.27 = (bf16[128,2,128]{2,0,1:T(8,128)(2,1)S(1)}, bf16[128,2,128]{2,0,1:T(8,128)(2,1)S(1)}, u32[]{:S(2)}, u32[]{:S(2)}) collective-permute-start(bf16[128,2,128]{2,0,1:T(8,128)(2,1)S(1)} %collective-permute-done.25), channel_id=1, source_target_pairs={{0,1},{1,2},{2,3},{3,4},{4,5},{5,6},{6,7},{7,8},{8,9},{9,10},{10,1... | collective-permute-start | bytes 196616 | tf_op jit(solution)/shard_map/ppermute | solution.py:75
  158.9 9.8 %collective-permute-start.28 = (bf16[128,2,128]{0,2,1:T(8,128)(2,1)S(1)}, bf16[128,2,128]{0,2,1:T(8,128)(2,1)S(1)}, u32[]{:S(2)}, u32[]{:S(2)}) collective-permute-start(bf16[128,2,128]{0,2,1:T(8,128)(2,1)S(1)} %collective-permute-done.26), channel_id=1, source_target_pairs={{0,1},{1,2},{2,3},{3,4},{4,5},{5,6},{6,7},{7,8},{8,9},{9,10},{10,1... | collective-permute-start | bytes 196616 | tf_op jit(solution)/shard_map/ppermute | solution.py:74
  161.4 9.8 %collective-permute-start.29 = (bf16[128,2,128]{2,0,1:T(8,128)(2,1)S(1)}, bf16[128,2,128]{2,0,1:T(8,128)(2,1)S(1)}, u32[]{:S(2)}, u32[]{:S(2)}) collective-permute-start(bf16[128,2,128]{2,0,1:T(8,128)(2,1)S(1)} %collective-permute-done.27), channel_id=1, source_target_pairs={{0,1},{1,2},{2,3},{3,4},{4,5},{5,6},{6,7},{7,8},{8,9},{9,10},{10,1... | collective-permute-start | bytes 196616 | tf_op jit(solution)/shard_map/ppermute | solution.py:75
  168.7 9.8 %collective-permute-start.30 = (bf16[128,2,128]{0,2,1:T(8,128)(2,1)S(1)}, bf16[128,2,128]{0,2,1:T(8,128)(2,1)S(1)}, u32[]{:S(2)}, u32[]{:S(2)}) collective-permute-start(bf16[128,2,128]{0,2,1:T(8,128)(2,1)S(1)} %collective-permute-done.28), channel_id=1, source_target_pairs={{0,1},{1,2},{2,3},{3,4},{4,5},{5,6},{6,7},{7,8},{8,9},{9,10},{10,1... | collective-permute-start | bytes 196616 | tf_op jit(solution)/shard_map/ppermute | solution.py:74
  171.2 19.6 %collective-permute-start.31 = (bf16[128,2,128]{2,0,1:T(8,128)(2,1)S(1)}, bf16[128,2,128]{2,0,1:T(8,128)(2,1)S(1)}, u32[]{:S(2)}, u32[]{:S(2)}) collective-permute-start(bf16[128,2,128]{2,0,1:T(8,128)(2,1)S(1)} %collective-permute-done.29), channel_id=1, source_target_pairs={{0,1},{1,2},{2,3},{3,4},{4,5},{5,6},{6,7},{7,8},{8,9},{9,10},{10,1... | collective-permute-start | bytes 196616 | tf_op jit(solution)/shard_map/ppermute | solution.py:75
  (3 other events, 24.8 us)
where the time goes:
time: 198 us; the launch traced here: 197 us
  waiting for transfers between devices  82.1 us (41%)
  starting transfers between devices  64.5 us (33%)
  matrix products  28.6 us (14%)
  local copies, waits for them, and re-layouts  15.6 us (8%)
  other arithmetic  4.56 us (2%)
    ppermute x16, waiting for transfers between devices, local_fn(): k_cur = lax.ppermute(k_cur, ('cpo', 'cpi'), shift_perm)  81.5 us
    ppermute x16, starting transfers between devices, local_fn(): v_cur = lax.ppermute(v_cur, ('cpo', 'cpi'), shift_perm)  33.8 us
    ppermute x16, starting transfers between devices, local_fn(): k_cur = lax.ppermute(k_cur, ('cpo', 'cpi'), shift_perm)  30.7 us
    unnamed x8, local copies, waits for them, and re-layouts  14.9 us
    dot_general x16, matrix products, attend_step(): jnp.einsum('kgts,skd->kgtd', exp_scores.astype(jnp.bfloat16), v_blk, pref...  8.29 us
    unnamed x2, matrix products  7.23 us
    dot_general x17, matrix products, attend_step(): jnp.einsum('tkgd,skd->kgts', q_grp, k_blk, preferred_element_type=jnp.flo...  6.11 us
    dot_general x1, matrix products, finish_output(): jnp.einsum('kgtd,kgde->te', attended, w_grp, preferred_element_type=jnp.f...  5.66 us
  transfers between devices with their start and end apart: 32, of which 16 were waited for; matrix products, arithmetic and copies ran while one was open for 20% of the time, Pallas kernels for 0%

commit v1 on v0

v1 whole, which is shorter than its diff:
```python
import functools
import math

import jax
import jax.numpy as jnp
import numpy as np
from jax import lax
from jax.experimental import pallas as pl
from jax.experimental.pallas import tpu as pltpu
from jax.sharding import PartitionSpec as P

WINDOW = 2048
ROPE_BASE = 10000.0
MESH = pl.DeviceIdType.MESH
F32, BF16 = jnp.float32, jnp.bfloat16
NEG = -jnp.inf


def rope_tables(tok_chip, n_chips, head_dim):
    half = head_dim // 2
    freq = ROPE_BASE ** (-np.arange(half, dtype=np.float64) * 2.0 / head_dim)
    local = np.arange(tok_chip, dtype=np.float64)[:, None] * freq
    base = (np.arange(n_chips, dtype=np.float64) * tok_chip)[:, None] * freq
    dup = lambda a: np.concatenate([a, a], axis=-1)
    loc = np.stack([dup(np.cos(local)), dup(np.sin(local))]).astype(np.float32)
    bas = np.stack([dup(np.cos(base)), dup(np.sin(base))]).astype(np.float32)
    return loc, bas


def kernel(dims, x_hbm, wq_hbm, wk_hbm, wv_hbm, wo_hbm, loc_hbm, bas_hbm, y_hbm,
           x2, wqr, wkr, wvr, wqb, wkvb, wob, loc, bas, f32a, f32b, own, kv, q_t, cs_t, m_s, l_s, acc, o_all, o_send, y_v, y_b,
           ld_sem, wq_sem, y_sem, xs_sem, xr_sem, ps_sem, pr_sem, ks_sem, kr_sem, os_sem, or_sem):
    n_outer, n_inner, tok, dm, g, hd, nb = dims
    n_chips = n_outer * n_inner // 2
    rank = lax.axis_index("cpo") * n_inner + lax.axis_index("cpi")
    c = lax.div(rank, 2)
    h = lax.rem(rank, 2)
    oh = 1 - h

    def dev(chip, core):
        r = chip * 2 + core
        return {"cpo": lax.div(r, n_inner), "cpi": lax.rem(r, n_inner)}

    def load(src, dst, sem):
        cp = pltpu.make_async_copy(src, dst, sem)
        cp.start()
        return cp

    barrier = pltpu.get_barrier_semaphore()
    pl.semaphore_signal(barrier, inc=1, device_id=dev(c, oh), device_id_type=MESH)
    for j in range(1, nb):
        @pl.when(c - j >= 0)
        def _():
            for hh in range(2):
                pl.semaphore_signal(barrier, inc=1, device_id=dev(c - j, hh), device_id_type=MESH)

    ld_x = load(x_hbm, x2.at[h], ld_sem.at[0])
    ld_k = load(wk_hbm, wkr, ld_sem.at[1])
    ld_v = load(wv_hbm, wvr, ld_sem.at[2])
    ld_l = load(loc_hbm, loc, ld_sem.at[3])
    ld_b = load(bas_hbm, bas, ld_sem.at[4])
    n_wq = wq_sem.shape[0]
    rows_wq = dm // n_wq
    head0 = pl.multiple_of(h * g, g)
    ld_q = [load(wq_hbm.at[pl.ds(i * rows_wq, rows_wq), pl.ds(head0, g), :], wqr.at[pl.ds(i * rows_wq, rows_wq)], wq_sem.at[i])
            for i in range(n_wq)]

    chunk = f32a.shape[0]
    for raw, ld, col in ((wkr, ld_k, 0), (wvr, ld_v, 1)):
        ld.wait()

        def relay_kv(i, _):
            r0 = pl.multiple_of(i * 2 * chunk, 2 * chunk)
            d0 = pl.multiple_of(i * chunk, chunk)
            for part, buf in enumerate((f32a, f32b)):
                buf[...] = raw[pl.ds(r0 + part * chunk, chunk), :].astype(F32)
                for hh in range(2):
                    piece = buf[pl.ds(hh, chunk // 2, stride=2), :].astype(BF16)
                    wkvb[pl.ds(d0 + part * (chunk // 2), chunk // 2), pl.ds((2 * hh + col) * hd, hd)] = piece
            return 0

        lax.fori_loop(0, 2 * dm // (2 * chunk), relay_kv, 0)

    ld_x.wait()
    n_tgt = jnp.minimum(nb - 1, n_chips - 1 - c)
    pl.semaphore_wait(barrier, 1 + 2 * n_tgt)
    x_copy = pltpu.make_async_remote_copy(src_ref=x2.at[h], dst_ref=x2.at[h], send_sem=xs_sem, recv_sem=xr_sem,
                                          device_id=dev(c, oh), device_id_type=MESH)
    x_copy.start()
    kvp = jnp.dot(x2[h], wkvb[...], preferred_element_type=F32)
    ld_l.wait()
    ld_b.wait()
    t0 = pl.multiple_of(h * tok, tok)
    cb, sb = bas[0, pl.ds(c, 1), :], bas[1, pl.ds(c, 1), :]
    cl, sl = loc[0, pl.ds(t0, tok), :], loc[1, pl.ds(t0, tok), :]
    cos_k = cl * cb - sl * sb
    sin_k = sl * cb + cl * sb
    lane = lax.broadcasted_iota(jnp.int32, (tok, hd), 1)
    sin_k = jnp.where(lane < hd // 2, -sin_k, sin_k)
    for hh in range(2):
        k = kvp[:, 2 * hh * hd:(2 * hh + 1) * hd]
        k = (k * cos_k + pltpu.roll(k, hd // 2, 1) * sin_k).astype(BF16)
        v = kvp[:, (2 * hh + 1) * hd:(2 * hh + 2) * hd]
        own[hh, 0] = k
        own[hh, 1] = v.T.astype(BF16)
    kv[0, h] = own[h]

    p_copy = pltpu.make_async_remote_copy(src_ref=own.at[oh], dst_ref=kv.at[0, h], send_sem=ps_sem, recv_sem=pr_sem,
                                          device_id=dev(c, oh), device_id_type=MESH)
    p_copy.start()

    def kv_copy(j, hh, chip):
        return pltpu.make_async_remote_copy(src_ref=own.at[hh], dst_ref=kv.at[j, h], send_sem=ks_sem.at[j, hh], recv_sem=kr_sem.at[j, h],
                                            device_id=dev(chip, hh), device_id_type=MESH)

    for j in range(1, nb):
        @pl.when(c + j < n_chips)
        def _():
            for hh in range(2):
                kv_copy(j, hh, c + j).start()

    ld_o = load(wo_hbm, wob, ld_sem.at[5])

    dch = chunk // g
    for i in range(n_wq):
        ld_q[i].wait()

        def relay_q(t, _):
            d0 = pl.multiple_of(i * rows_wq + t * 2 * dch, 2 * dch)
            for part, buf in enumerate((f32a, f32b)):
                dd = pl.multiple_of(d0 + part * dch, dch)
                buf[...] = wqr[pl.ds(dd, dch)].astype(F32).reshape(chunk, hd)
                for n in range(g):
                    wqb[pl.ds(dd, dch), n * hd:(n + 1) * hd] = buf[pl.ds(n, dch, stride=g), :].astype(BF16)
            return 0

        lax.fori_loop(0, rows_wq // (2 * dch), relay_q, 0)
    half = hd // 2
    cl, sl = loc[0], loc[1]
    cs_t[0] = (cl * cb - sl * sb).T[:half]
    cs_t[1] = (sl * cb + cl * sb).T[:half]
    x_copy.wait_recv()
    xall = x2[...].reshape(2 * tok, dm)

    def proj_q(n, _):
        c0 = pl.multiple_of(n * 2 * hd, 2 * hd)
        qp = jnp.dot(xall, wqb[:, pl.ds(c0, 2 * hd)], preferred_element_type=F32)
        for s in range(2):
            qt = qp[:, s * hd:(s + 1) * hd].T
            lo, hi = qt[:half], qt[half:]
            q_t[2 * n + s, :half] = (lo * cs_t[0] - hi * cs_t[1]).astype(BF16)
            q_t[2 * n + s, half:] = (hi * cs_t[0] + lo * cs_t[1]).astype(BF16)
        return 0

    lax.fori_loop(0, g // 2, proj_q, 0)

    scale = hd ** -0.5 * math.log2(math.e)
    ki = lax.broadcasted_iota(jnp.int32, (2 * tok, 2 * tok), 0)
    qi = lax.broadcasted_iota(jnp.int32, (2 * tok, 2 * tok), 1)

    def attend(j):
        def head(n, _):
            kb = kv[j, :, 0].reshape(2 * tok, hd)
            vb = jnp.concatenate([kv[j, 0, 1], kv[j, 1, 1]], axis=1)
            s = jnp.dot(kb, q_t[n], preferred_element_type=F32) * scale
            if j == 0:
                s = jnp.where(ki <= qi, s, NEG)
            if j == nb - 1:
                s = jnp.where(ki > qi, s, NEG)
            top = jnp.max(s, axis=0, keepdims=True)
            if j == 0:
                m_new = top
                p = jnp.exp2(s - m_new)
                l_s[n] = jnp.sum(p, axis=0, keepdims=True)
                acc[n] = jnp.dot(vb, p.astype(BF16), preferred_element_type=F32)
            else:
                m_old = m_s[n]
                m_new = jnp.maximum(m_old, top)
                p = jnp.exp2(s - m_new)
                alpha = jnp.exp2(m_old - m_new)
                l_s[n] = l_s[n] * alpha + jnp.sum(p, axis=0, keepdims=True)
                acc[n] = acc[n] * alpha + jnp.dot(vb, p.astype(BF16), preferred_element_type=F32)
            m_s[n] = m_new
            return 0

        lax.fori_loop(0, g, head, 0)

    p_copy.wait_recv()
    attend(0)
    for j in range(1, nb):
        @pl.when(c - j >= 0)
        def _():
            for s in range(2):
                pltpu.make_async_copy(own.at[0], kv.at[j, s], kr_sem.at[j, s]).wait()
            attend(j)

    def finish(n, _):
        o = (acc[n] / l_s[n]).T.astype(BF16)
        c0 = pl.multiple_of(n * hd, hd)
        o_send[0, :, pl.ds(c0, hd)] = o[:tok]
        o_send[1, :, pl.ds(c0, hd)] = o[tok:]
        return 0

    lax.fori_loop(0, g, finish, 0)
    o_copy = pltpu.make_async_remote_copy(src_ref=o_send.at[oh], dst_ref=o_all, send_sem=os_sem, recv_sem=or_sem,
                                          device_id=dev(c, oh), device_id_type=MESH)
    o_copy.start()
    ld_o.wait()
    w0 = pl.multiple_of(h * g * hd, g * hd)
    w1 = pl.multiple_of(oh * g * hd, g * hd)
    o_own = o_send[h]
    n_y = y_sem.shape[0]
    cols = dm // n_y

    def own_part(i, _):
        c0 = pl.multiple_of(i * cols, cols)
        y_v[:, pl.ds(c0, cols)] = jnp.dot(o_own, wob[pl.ds(w0, g * hd), pl.ds(c0, cols)], preferred_element_type=F32)
        return 0

    lax.fori_loop(0, n_y, own_part, 0)
    o_copy.wait_recv()
    o_oth = o_all[...]
    outs = []
    for i in range(n_y):
        cs = slice(i * cols, (i + 1) * cols)
        y_b[:, cs] = (y_v[:, cs] + jnp.dot(o_oth, wob[pl.ds(w1, g * hd), cs], preferred_element_type=F32)).astype(BF16)
        outs.append(load(y_b.at[:, cs], y_hbm.at[:, cs], y_sem.at[i]))
    for cp in outs:
        cp.wait()
    x_copy.wait_send()
    p_copy.wait_send()
    o_copy.wait_send()
    for j in range(1, nb):
        @pl.when(c + j < n_chips)
        def _():
            for hh in range(2):
                kv_copy(j, hh, c + j).wait_send()


def solution(mesh):
    n_outer, n_inner = mesh.shape['cpo'], mesh.shape['cpi']

    def local_fn(hidden, w_q, w_k, w_v, w_o):
        tok, dm = hidden.shape
        hq, hd = w_q.shape[1], w_q.shape[2]
        g = hq // 2
        nb = WINDOW // (2 * tok) + 1
        loc, bas = rope_tables(2 * tok, n_outer * n_inner // 2, hd)
        dims = (n_outer, n_inner, tok, dm, g, hd, nb)
        chunk = 1024
        scratch = [
            pltpu.VMEM((2, tok, dm), BF16), pltpu.VMEM((dm, g, hd), BF16), pltpu.VMEM((2 * dm, hd), BF16), pltpu.VMEM((2 * dm, hd), BF16),
            pltpu.VMEM((dm, g * hd), BF16), pltpu.VMEM((dm, 4 * hd), BF16), pltpu.VMEM((hq * hd, dm), BF16),
            pltpu.VMEM(loc.shape, F32), pltpu.VMEM(bas.shape, F32),
            pltpu.VMEM((chunk, hd), F32), pltpu.VMEM((chunk, hd), F32),
            pltpu.VMEM((2, 2, tok, hd), BF16), pltpu.VMEM((nb, 2, 2, tok, hd), BF16),
            pltpu.VMEM((g, hd, 2 * tok), BF16), pltpu.VMEM((2, hd // 2, 2 * tok), F32),
            pltpu.VMEM((g, 1, 2 * tok), F32), pltpu.VMEM((g, 1, 2 * tok), F32), pltpu.VMEM((g, hd, 2 * tok), F32),
            pltpu.VMEM((tok, g * hd), BF16), pltpu.VMEM((2, tok, g * hd), BF16), pltpu.VMEM((tok, dm), F32), pltpu.VMEM((tok, dm), BF16),
            pltpu.SemaphoreType.DMA((6,)), pltpu.SemaphoreType.DMA((4,)), pltpu.SemaphoreType.DMA((4,)),
            pltpu.SemaphoreType.DMA, pltpu.SemaphoreType.DMA, pltpu.SemaphoreType.DMA, pltpu.SemaphoreType.DMA,
            pltpu.SemaphoreType.DMA((nb, 2)), pltpu.SemaphoreType.DMA((nb, 2)), pltpu.SemaphoreType.DMA, pltpu.SemaphoreType.DMA,
        ]
        return pl.pallas_call(
            functools.partial(kernel, dims),
            out_shape=jax.ShapeDtypeStruct((tok, dm), BF16),
            in_specs=[pl.BlockSpec(memory_space=pl.ANY)] * 7,
            out_specs=pl.BlockSpec(memory_space=pl.ANY),
            scratch_shapes=scratch,
            compiler_params=pltpu.CompilerParams(collective_id=0, has_side_effects=True, vmem_limit_bytes=56 * 1024 * 1024),
        )(hidden, w_q, w_k.reshape(2 * dm, hd), w_v.reshape(2 * dm, hd), w_o.reshape(hq * hd, dm), jnp.asarray(loc), jnp.asarray(bas))

    return jax.shard_map(local_fn, mesh=mesh,
                         in_specs=(P(('dp', 'cpo', 'cpi'), None), P(), P(), P(), P()),
                         out_specs=P(('dp', 'cpo', 'cpi'), None), check_vma=False)
```

time: 198 us -> 52 us (0.26)
  the two profiles are of different devices: /device:TPU:96 before, /device:TPU:65 now
where the time goes in v1:
time: 52 us; the launch traced here: 51.8 us
  Pallas kernels  49.9 us (96%)
  local copies, waits for them, and re-layouts  1.88 us (4%)
    pallas_call x1, Pallas kernels, local_fn(): pl.pallas_call(functools.partial(kernel, dims), out_shape=jax.ShapeDtypeS...  49.9 us
    unnamed x1, local copies, waits for them, and re-layouts  1.88 us

profile of v1, /device:TPU:65, one launch (start us, length us, event | category | flops | bytes accessed | tf_op | source)
XLA Modules:
  0.0 51.8 jit_solution(11378164058894959927)
XLA Ops:
  0.0 49.9 %shard_map.73 = bf16[128,2048]{1,0:T(8,128)(2,1)} custom-call(bf16[128,2048]{1,0:T(8,128)(2,1)} %x_hbm.1, bf16[2048,16,128]{2,1,0:T(8,128)(2,1)} %wq_hbm.1, bf16[4096,128]{1,0:T(8,128)(2,1)} %bitcast.4, bf16[4096,128]{1,0:T(8,128)(2,1)} %bitcast.5, bf16[2048,2048]{1,0:T(8,128)(2,1)} %bitcast.3, f32[2,256,128]{2,1,0:T(8,128)} %constant.4.clone.loc_hbm, ...), custom_call_target="tpu_custom_call" | custom-call | tf_op jit(solution)/shard_map/pallas_call | solution.py:264
  49.9 1.9 %copy.9 = bf16[128,2048]{1,0:T(8,128)(2,1)} copy(bf16[128,2048]{1,0:T(8,128)(2,1)} %shard_map.73) | data formatting | bytes 1048576

commit v2 on v1

v2 whole, which is shorter than its diff:
```python
import functools
import math

import jax
import jax.numpy as jnp
import numpy as np
from jax import lax
from jax.experimental import pallas as pl
from jax.experimental.pallas import tpu as pltpu
from jax.sharding import PartitionSpec as P

WINDOW = 2048
ROPE_BASE = 10000.0
MESH = pl.DeviceIdType.MESH
F32, BF16 = jnp.float32, jnp.bfloat16


def rope_tables(tok_chip, n_chips, head_dim):
    half = head_dim // 2
    freq = ROPE_BASE ** (-np.arange(half, dtype=np.float64) * 2.0 / head_dim)
    local = np.arange(tok_chip, dtype=np.float64)[:, None] * freq
    base = (np.arange(n_chips, dtype=np.float64) * tok_chip)[:, None] * freq
    dup = lambda a: np.concatenate([a, a], axis=-1)
    loc = np.stack([dup(np.cos(local)), dup(np.sin(local))]).astype(np.float32)
    bas = np.stack([dup(np.cos(base)), dup(np.sin(base))]).astype(np.float32)
    return loc, bas


def kernel(dims, x_hbm, wq_hbm, wk_hbm, wv_hbm, wo_hbm, loc_hbm, bas_hbm, y_hbm,
           x2, wqr, wkr, wvr, wqb, wkvb, wob, loc, bas, f32a, f32b, own, kv, q_t, cs_t, m_s, l_s, acc, o_all, o_send, y_v, y_b,
           ld_sem, wq_sem, y_sem, xs_sem, xr_sem, ps_sem, pr_sem, ks_sem, kr_sem, rs_sem, rr_sem, os_sem, or_sem):
    n_outer, n_inner, tok, dm, g, hd, nb = dims
    n_row = n_inner // 2
    n_chips = n_outer * n_inner // 2
    rank = lax.axis_index("cpo") * n_inner + lax.axis_index("cpi")
    c = lax.div(rank, 2)
    h = lax.rem(rank, 2)
    oh = 1 - h

    def dev(chip, core):
        r = chip * 2 + core
        return {"cpo": lax.div(r, n_inner), "cpi": lax.rem(r, n_inner)}

    def load(src, dst, sem):
        cp = pltpu.make_async_copy(src, dst, sem)
        cp.start()
        return cp

    row, col = lax.div(c, n_row), lax.rem(c, n_row)
    n_rows = n_chips // n_row
    last = nb - 1


    barrier = pltpu.get_barrier_semaphore()

    def greet(chip, core):
        pl.semaphore_signal(barrier, inc=1, device_id=dev(chip, core), device_id_type=MESH)

    right = row * n_row + lax.rem(col + 1, n_row)
    left = row * n_row + lax.rem(col + n_row - 1, n_row)
    one = lambda cond: jnp.where(cond, 1, 0)
    both = jnp.logical_and
    up1, up2, dn1, dn2 = row + 1 < n_rows, row + 2 < n_rows, row >= 1, row >= 2

    odd = lax.rem(row, 2) == 1
    direct = [(up1, 4, c + 4), (col < 3, 1, c + 1), (col < 1, 3, c + 3), (col < 2, 2, c + 2), (both(up2, odd), 8, c + 8)]
    later = [(both(up2, jnp.logical_not(odd)), 8, c + 8), (both(up1, col == 3), 5, c + 1)]
    origin = [(dn1, c - 4), (col >= 1, c - 1), (both(dn1, col == 0), c - 1), (dn2, c - 8), (col >= 3, c - 3), (col >= 2, c - 2)]
    relay_row = [(both(dn1, col < 3), 4, 5, right), (dn1, 4, 7, left)]
    relay_far = [(both(dn2, col >= 1), 8, 3, left), (both(dn2, col == 3), 8, 1, right), (both(dn2, col >= 2), 8, 2, c - 2)]
    relay_5 = [(both(dn1, col < 2), 5, 6, right)]
    relay_7 = [(both(dn1, col < 2), 7, 6, left)]

    def when_all(cond, act):
        pl.when(cond)(act)

    greet(c, oh)
    for cond, chip in origin:
        when_all(cond, lambda chip=chip: [greet(chip, hh) for hh in range(2)] and None)
    when_all(dn1, lambda: [greet(chip, h) for chip in (left, right)] and None)
    when_all(both(dn2, col < 2), lambda: greet(c + 2, h))
    n_sent = 1 + 2 * one(dn1) + one(both(dn2, col >= 2))
    for cond, _, _ in direct + later:
        n_sent = n_sent + 2 * one(cond)

    ld_x = load(x_hbm, x2.at[h], ld_sem.at[0])
    ld_k = load(wk_hbm, wkr, ld_sem.at[1])
    ld_v = load(wv_hbm, wvr, ld_sem.at[2])
    ld_l = load(loc_hbm, loc, ld_sem.at[3])
    ld_b = load(bas_hbm, bas, ld_sem.at[4])
    chunk = f32a.shape[0]
    with jax.named_scope("relay_kv"):
        for raw, ld, sel in ((wkr, ld_k, 0), (wvr, ld_v, 1)):
            ld.wait()

            def relay_kv(i, _):
                r0 = pl.multiple_of(i * 2 * chunk, 2 * chunk)
                d0 = pl.multiple_of(i * chunk, chunk)
                for part, buf in enumerate((f32a, f32b)):
                    buf[...] = raw[pl.ds(r0 + part * chunk, chunk), :].astype(F32)
                    for hh in range(2):
                        piece = buf[pl.ds(hh, chunk // 2, stride=2), :].astype(BF16)
                        wkvb[pl.ds(d0 + part * (chunk // 2), chunk // 2), pl.ds((2 * hh + sel) * hd, hd)] = piece
                return 0

            lax.fori_loop(0, 2 * dm // (2 * chunk), relay_kv, 0)
    n_wq = wq_sem.shape[0]
    rows_wq = dm // n_wq
    head0 = pl.multiple_of(h * g, g)
    ld_q = [load(wq_hbm.at[pl.ds(i * rows_wq, rows_wq), pl.ds(head0, g), :], wqr.at[pl.ds(i * rows_wq, rows_wq)], wq_sem.at[i])
            for i in range(n_wq)]

    ld_x.wait()
    with jax.named_scope("kvproj"):
        kvp = jnp.dot(x2[h], wkvb[...], preferred_element_type=F32)
    ld_l.wait()
    ld_b.wait()
    t0 = pl.multiple_of(h * tok, tok)
    cb, sb = bas[0, pl.ds(c, 1), :], bas[1, pl.ds(c, 1), :]
    cl, sl = loc[0, pl.ds(t0, tok), :], loc[1, pl.ds(t0, tok), :]
    cos_k = cl * cb - sl * sb
    sin_k = sl * cb + cl * sb
    lane = lax.broadcasted_iota(jnp.int32, (tok, hd), 1)
    sin_k = jnp.where(lane < hd // 2, -sin_k, sin_k)
    for hh in range(2):
        k = kvp[:, 2 * hh * hd:(2 * hh + 1) * hd]
        k = (k * cos_k + pltpu.roll(k, hd // 2, 1) * sin_k).astype(BF16)
        v = kvp[:, (2 * hh + 1) * hd:(2 * hh + 2) * hd]
        own[hh, 0] = k
        own[hh, 1] = v.T.astype(BF16)
    kv[0, h] = own[h]

    with jax.named_scope("barrier"):
        pl.semaphore_wait(barrier, n_sent)
    x_copy = pltpu.make_async_remote_copy(src_ref=x2.at[h], dst_ref=x2.at[h], send_sem=xs_sem, recv_sem=xr_sem,
                                          device_id=dev(c, oh), device_id_type=MESH)

    p_copy = pltpu.make_async_remote_copy(src_ref=own.at[oh], dst_ref=kv.at[0, h], send_sem=ps_sem, recv_sem=pr_sem,
                                          device_id=dev(c, oh), device_id_type=MESH)
    p_copy.start()

    def each_direct(act, first, group):
        for i, (cond, slot, chip) in enumerate(group, first):
            @pl.when(cond)
            def _():
                for hh in range(2):
                    act(pltpu.make_async_remote_copy(src_ref=own.at[hh], dst_ref=kv.at[slot, h], send_sem=ks_sem.at[i, hh],
                                                     recv_sem=kr_sem.at[slot, h], device_id=dev(chip, hh), device_id_type=MESH))

    relays = relay_row + relay_far + relay_5 + relay_7

    def each_relay(act, group):
        for item in group:
            cond, src, dst, chip = item
            i = [r is item for r in relays].index(True)

            @pl.when(cond)
            def _():
                act(pltpu.make_async_remote_copy(src_ref=kv.at[src], dst_ref=kv.at[dst], send_sem=rs_sem.at[i], recv_sem=rr_sem.at[dst],
                                                 device_id=dev(chip, h), device_id_type=MESH))

    each_direct(lambda cp: cp.start(), 0, direct)
    x_copy.start()

    ld_o = load(wo_hbm, wob, ld_sem.at[5])

    with jax.named_scope("relay_q"):
        dch = chunk // g
        for i in range(n_wq):
            ld_q[i].wait()

            def relay_q(t, _):
                d0 = pl.multiple_of(i * rows_wq + t * 2 * dch, 2 * dch)
                for part, buf in enumerate((f32a, f32b)):
                    dd = pl.multiple_of(d0 + part * dch, dch)
                    buf[...] = wqr[pl.ds(dd, dch)].astype(F32).reshape(chunk, hd)
                    for n in range(g):
                        wqb[pl.ds(dd, dch), n * hd:(n + 1) * hd] = buf[pl.ds(n, dch, stride=g), :].astype(BF16)
                return 0

            lax.fori_loop(0, rows_wq // (2 * dch), relay_q, 0)
    each_direct(lambda cp: cp.start(), len(direct), later)
    half = hd // 2
    cl, sl = loc[0], loc[1]
    cs_t[0] = (cl * cb - sl * sb).T[:half]
    cs_t[1] = (sl * cb + cl * sb).T[:half]
    with jax.named_scope("xwait"):
        x_copy.wait_recv()
    xall = x2[...].reshape(2 * tok, dm)

    def proj_q(n, _):
        c0 = pl.multiple_of(n * 2 * hd, 2 * hd)
        qp = jnp.dot(xall, wqb[:, pl.ds(c0, 2 * hd)], preferred_element_type=F32)
        for s in range(2):
            qt = qp[:, s * hd:(s + 1) * hd].T
            lo, hi = qt[:half], qt[half:]
            q_t[2 * n + s, :half] = (lo * cs_t[0] - hi * cs_t[1]).astype(BF16)
            q_t[2 * n + s, half:] = (hi * cs_t[0] + lo * cs_t[1]).astype(BF16)
        return 0

    with jax.named_scope("qproj"):
        lax.fori_loop(0, g // 2, proj_q, 0)
    scale = hd ** -0.5 * math.log2(math.e)
    ki = lax.broadcasted_iota(jnp.int32, (2 * tok, 2 * tok), 0)
    qi = lax.broadcasted_iota(jnp.int32, (2 * tok, 2 * tok), 1)

    def attend(slot):
        kb = kv[slot, :, 0].reshape(2 * tok, hd)
        vb = jnp.concatenate([kv[slot, 0, 1], kv[slot, 1, 1]], axis=1)

        def weigh(n, s):
            if slot == 0:
                s = jnp.where(ki <= qi, s, -jnp.inf)
            if slot == last:
                s = jnp.where(ki > qi, s, -jnp.inf)
            top = jnp.max(s, axis=0, keepdims=True) * scale
            m_new = top if slot == 0 else jnp.maximum(m_s[n], top)
            p = jnp.exp2(s * scale - m_new)
            tot = jnp.sum(p, axis=0, keepdims=True)
            alpha = None
            if slot == 0:
                l_s[n] = tot
            else:
                alpha = jnp.exp2(m_s[n] - m_new)
                l_s[n] = l_s[n] * alpha + tot
            m_s[n] = m_new
            return p.astype(BF16), alpha

        def gather(n, p, alpha):
            r = jnp.dot(vb, p, preferred_element_type=F32)
            acc[n] = r if alpha is None else acc[n] * alpha + r

        scores, held = [], None
        for n in range(g):
            while len(scores) < min(n + 3, g):
                scores.append(jnp.dot(kb, q_t[len(scores)], preferred_element_type=F32))
            p, alpha = weigh(n, scores[n])
            if held is not None:
                gather(*held)
            held = (n, p, alpha)
        gather(*held)

    def landed(slot, relayed):
        with jax.named_scope(f"w{slot}{'r' * relayed}"):
            if relayed:
                pltpu.make_async_copy(kv.at[0], kv.at[slot], rr_sem.at[slot]).wait()
            else:
                for s in range(2):
                    pltpu.make_async_copy(own.at[0], kv.at[slot, s], kr_sem.at[slot, s]).wait()

    def visit(slot, here, relay=(), got=False, direct_if=None, relayed=False):
        @pl.when(here)
        def _():
            if not got:
                if direct_if is None:
                    landed(slot, relayed)
                else:
                    pl.when(direct_if)(lambda: landed(slot, False))
                    pl.when(jnp.logical_not(direct_if))(lambda: landed(slot, True))
                each_relay(lambda cp: cp.start(), relay)
            with jax.named_scope(f"att{slot}"):
                attend(slot)

    def first_relay(late):
        @pl.when(both(dn1, (lax.rem(row, 4) == 0) == late))
        def _():
            landed(4, False)
            each_relay(lambda cp: cp.start(), relay_row)

    first_relay(False)
    with jax.named_scope("pwait"):
        p_copy.wait_recv()
    with jax.named_scope("att0"):
        attend(0)
    first_relay(True)
    visit(4, dn1, got=True)
    visit(1, col >= 1)
    visit(8, dn2, relay=relay_far)
    visit(2, col >= 2)
    visit(3, col >= 3)
    visit(5, dn1, relay=relay_5, direct_if=col == 0)
    visit(7, dn1, relay=relay_7, relayed=True)
    visit(3, both(dn2, col < 3), relayed=True)
    visit(6, dn1, relayed=True)
    visit(1, both(dn2, col < 1), relayed=True)
    visit(2, both(dn2, col < 2), relayed=True)

    def finish(n, _):
        o = (acc[n] / l_s[n]).T.astype(BF16)
        c0 = pl.multiple_of(n * hd, hd)
        o_send[0, :, pl.ds(c0, hd)] = o[:tok]
        o_send[1, :, pl.ds(c0, hd)] = o[tok:]
        return 0

    with jax.named_scope("finish"):
        lax.fori_loop(0, g, finish, 0, unroll=True)
    o_copy = pltpu.make_async_remote_copy(src_ref=o_send.at[oh], dst_ref=o_all, send_sem=os_sem, recv_sem=or_sem,
                                          device_id=dev(c, oh), device_id_type=MESH)
    o_copy.start()
    with jax.named_scope("wowait"):
        ld_o.wait()
    w0 = pl.multiple_of(h * g * hd, g * hd)
    w1 = pl.multiple_of(oh * g * hd, g * hd)
    o_own = o_send[h]
    n_y = y_sem.shape[0]
    cols = dm // n_y

    def own_part(i, _):
        c0 = pl.multiple_of(i * cols, cols)
        y_v[:, pl.ds(c0, cols)] = jnp.dot(o_own, wob[pl.ds(w0, g * hd), pl.ds(c0, cols)], preferred_element_type=F32)
        return 0

    with jax.named_scope("wo_own"):
        lax.fori_loop(0, n_y, own_part, 0)
    with jax.named_scope("owait"):
        o_copy.wait_recv()
    o_oth = o_all[...]
    outs = []
    with jax.named_scope("wo_oth"):
        for i in range(n_y):
            cs = slice(i * cols, (i + 1) * cols)
            y_b[:, cs] = (y_v[:, cs] + jnp.dot(o_oth, wob[pl.ds(w1, g * hd), cs], preferred_element_type=F32)).astype(BF16)
            outs.append(load(y_b.at[:, cs], y_hbm.at[:, cs], y_sem.at[i]))
    with jax.named_scope("ywait"):
        for cp in outs:
            cp.wait()
    with jax.named_scope("sendwait"):
        x_copy.wait_send()
        p_copy.wait_send()
        o_copy.wait_send()
        each_direct(lambda cp: cp.wait_send(), 0, direct + later)

        each_relay(lambda cp: cp.wait_send(), relays)


def solution(mesh):
    n_outer, n_inner = mesh.shape['cpo'], mesh.shape['cpi']

    def local_fn(hidden, w_q, w_k, w_v, w_o):
        tok, dm = hidden.shape
        hq, hd = w_q.shape[1], w_q.shape[2]
        g = hq // 2
        nb = WINDOW // (2 * tok) + 1
        loc, bas = rope_tables(2 * tok, n_outer * n_inner // 2, hd)
        dims = (n_outer, n_inner, tok, dm, g, hd, nb)
        chunk = 1024
        scratch = [
            pltpu.VMEM((2, tok, dm), BF16), pltpu.VMEM((dm, g, hd), BF16), pltpu.VMEM((2 * dm, hd), BF16), pltpu.VMEM((2 * dm, hd), BF16),
            pltpu.VMEM((dm, g * hd), BF16), pltpu.VMEM((dm, 4 * hd), BF16), pltpu.VMEM((hq * hd, dm), BF16),
            pltpu.VMEM(loc.shape, F32), pltpu.VMEM(bas.shape, F32),
            pltpu.VMEM((chunk, hd), F32), pltpu.VMEM((chunk, hd), F32),
            pltpu.VMEM((2, 2, tok, hd), BF16), pltpu.VMEM((nb, 2, 2, tok, hd), BF16),
            pltpu.VMEM((g, hd, 2 * tok), BF16), pltpu.VMEM((2, hd // 2, 2 * tok), F32),
            pltpu.VMEM((g, 1, 2 * tok), F32), pltpu.VMEM((g, 1, 2 * tok), F32), pltpu.VMEM((g, hd, 2 * tok), F32),
            pltpu.VMEM((tok, g * hd), BF16), pltpu.VMEM((2, tok, g * hd), BF16), pltpu.VMEM((tok, dm), F32), pltpu.VMEM((tok, dm), BF16),
            pltpu.SemaphoreType.DMA((6,)), pltpu.SemaphoreType.DMA((4,)), pltpu.SemaphoreType.DMA((4,)),
            pltpu.SemaphoreType.DMA, pltpu.SemaphoreType.DMA, pltpu.SemaphoreType.DMA, pltpu.SemaphoreType.DMA,
            pltpu.SemaphoreType.DMA((2 * nb, 2)), pltpu.SemaphoreType.DMA((nb, 2)), *[pltpu.SemaphoreType.DMA((nb,))] * 2, pltpu.SemaphoreType.DMA, pltpu.SemaphoreType.DMA,
        ]
        return pl.pallas_call(
            functools.partial(kernel, dims),
            out_shape=jax.ShapeDtypeStruct((tok, dm), BF16),
            in_specs=[pl.BlockSpec(memory_space=pl.ANY)] * 7,
            out_specs=pl.BlockSpec(memory_space=pl.ANY),
            scratch_shapes=scratch,
            compiler_params=pltpu.CompilerParams(collective_id=0, has_side_effects=True, vmem_limit_bytes=56 * 1024 * 1024),
        )(hidden, w_q, w_k.reshape(2 * dm, hd), w_v.reshape(2 * dm, hd), w_o.reshape(hq * hd, dm), jnp.asarray(loc), jnp.asarray(bas))

    return jax.shard_map(local_fn, mesh=mesh,
                         in_specs=(P(('dp', 'cpo', 'cpi'), None), P(), P(), P(), P()),
                         out_specs=P(('dp', 'cpo', 'cpi'), None), check_vma=False)
```

time: 52 us -> 30.2 us (0.58)
  the two profiles are of different devices: /device:TPU:65 before, /device:TPU:33 now
where the time goes in v2:
time: 30.2 us; the launch traced here: 30 us
  Pallas kernels  28.2 us (93%)
  local copies, waits for them, and re-layouts  1.88 us (6%)
    pallas_call x1, Pallas kernels, local_fn(): pl.pallas_call(functools.partial(kernel, dims), out_shape=jax.ShapeDtypeS...  28.2 us
    unnamed x1, local copies, waits for them, and re-layouts  1.88 us

profile of v2, /device:TPU:33, one launch (start us, length us, event | category | flops | bytes accessed | tf_op | source)
XLA Modules:
  0.0 30.0 jit_solution(16614779383363572472)
XLA Ops:
  0.0 28.2 %shard_map.73 = bf16[128,2048]{1,0:T(8,128)(2,1)} custom-call(bf16[128,2048]{1,0:T(8,128)(2,1)} %x_hbm.1, bf16[2048,16,128]{2,1,0:T(8,128)(2,1)} %wq_hbm.1, bf16[4096,128]{1,0:T(8,128)(2,1)} %bitcast.4, bf16[4096,128]{1,0:T(8,128)(2,1)} %bitcast.5, bf16[2048,2048]{1,0:T(8,128)(2,1)} %bitcast.3, f32[2,256,128]{2,1,0:T(8,128)} %constant.4.clone.loc_hbm, ...), custom_call_target="tpu_custom_call" | custom-call | tf_op jit(solution)/shard_map/pallas_call | solution.py:360
  28.2 1.9 %copy.9 = bf16[128,2048]{1,0:T(8,128)(2,1)} copy(bf16[128,2048]{1,0:T(8,128)(2,1)} %shard_map.73) | data formatting | bytes 1048576

commit v3 on v2

v3 whole, which is shorter than its diff:
```python
import functools
import math

import jax
import jax.numpy as jnp
import numpy as np
from jax import lax
from jax.experimental import pallas as pl
from jax.experimental.pallas import tpu as pltpu
from jax.sharding import PartitionSpec as P

WINDOW = 2048
ROPE_BASE = 10000.0
MESH = pl.DeviceIdType.MESH
F32, BF16 = jnp.float32, jnp.bfloat16


def rope_tables(tok_chip, n_chips, head_dim):
    half = head_dim // 2
    freq = ROPE_BASE ** (-np.arange(half, dtype=np.float64) * 2.0 / head_dim)
    local = np.arange(tok_chip, dtype=np.float64)[:, None] * freq
    base = (np.arange(n_chips, dtype=np.float64) * tok_chip)[:, None] * freq
    dup = lambda a: np.concatenate([a, a], axis=-1)
    loc = np.stack([dup(np.cos(local)), dup(np.sin(local))]).astype(np.float32)
    bas = np.stack([dup(np.cos(base)), dup(np.sin(base))]).astype(np.float32)
    return loc, bas


def kernel(dims, x_hbm, wq_hbm, wk_hbm, wv_hbm, wo_hbm, loc_hbm, bas_hbm, y_ref,
           x2, wqr, wkr, wvr, big, wob, loc, bas, own, kv, q_t, cs_t, m_s, l_s, acc, o_all, o_send, y_v,
           ld_sem, wq_sem, xs_sem, xr_sem, ps_sem, pr_sem, ks_sem, kr_sem, rs_sem, rr_sem, os_sem, or_sem):
    n_outer, n_inner, tok, dm, g, hd, nb = dims
    n_row = n_inner // 2
    n_chips = n_outer * n_inner // 2
    rank = lax.axis_index("cpo") * n_inner + lax.axis_index("cpi")
    c = lax.div(rank, 2)
    h = lax.rem(rank, 2)
    oh = 1 - h

    def dev(chip, core):
        r = chip * 2 + core
        return {"cpo": lax.div(r, n_inner), "cpi": lax.rem(r, n_inner)}

    def load(src, dst, sem):
        cp = pltpu.make_async_copy(src, dst, sem)
        cp.start()
        return cp

    row, col = lax.div(c, n_row), lax.rem(c, n_row)
    n_rows = n_chips // n_row
    last = nb - 1


    barrier = pltpu.get_barrier_semaphore()

    def greet(chip, core):
        pl.semaphore_signal(barrier, inc=1, device_id=dev(chip, core), device_id_type=MESH)

    right = row * n_row + lax.rem(col + 1, n_row)
    left = row * n_row + lax.rem(col + n_row - 1, n_row)
    one = lambda cond: jnp.where(cond, 1, 0)
    both = jnp.logical_and
    up1, up2, dn1, dn2 = row + 1 < n_rows, row + 2 < n_rows, row >= 1, row >= 2

    odd = lax.rem(row, 2) == 1
    direct = [(up1, 4, c + 4), (col < 3, 1, c + 1), (col < 1, 3, c + 3), (col < 2, 2, c + 2), (both(up2, odd), 8, c + 8)]
    edge = lax.rem(row, 4) == 0
    later = [(both(up2, edge), 8, c + 8)]
    origin = [(dn1, c - 4), (col >= 1, c - 1), (both(dn2, jnp.logical_not(edge)), c - 8), (col >= 3, c - 3), (col >= 2, c - 2)]
    relay_row = [(dn1, 4, 5, right), (dn1, 4, 7, left), (both(dn1, both(up1, lax.rem(row, 4) == 3)), 4, 8, c + 4)]
    relay_far = [(both(dn2, col >= 1), 8, 3, left), (both(dn2, col == 3), 8, 1, right), (both(dn2, col >= 2), 8, 2, c - 2)]
    relay_5 = [(both(dn1, col < 2), 5, 6, right)]
    relay_7 = [(both(dn1, col < 2), 7, 6, left)]

    def when_all(cond, act):
        pl.when(cond)(act)

    greet(c, oh)
    for cond, chip in origin:
        when_all(cond, lambda chip=chip: [greet(chip, hh) for hh in range(2)] and None)
    when_all(dn1, lambda: [greet(chip, h) for chip in (left, right)] and None)
    when_all(both(dn2, col < 2), lambda: greet(c + 2, h))
    n_sent = 1 + 2 * one(dn1) + one(both(dn2, col >= 2))
    for cond, _, _ in direct + later:
        n_sent = n_sent + 2 * one(cond)

    ld_x = load(x_hbm, x2.at[h], ld_sem.at[0])
    ld_k = [load(wk_hbm.at[pl.ds(i * dm, dm)], wkr.at[pl.ds(i * dm, dm)], ld_sem.at[1 + i]) for i in range(2)]
    ld_v = [load(wv_hbm.at[pl.ds(i * dm, dm)], wvr.at[pl.ds(i * dm, dm)], ld_sem.at[6 + i]) for i in range(2)]
    ld_l = load(loc_hbm, loc, ld_sem.at[3])
    ld_b = load(bas_hbm, bas, ld_sem.at[4])
    def unpack(src, dst_row, rows):
        step = 1024

        def body(t, _):
            r = pl.multiple_of(t * step, step)
            big[pl.ds(pl.multiple_of(dst_row + r, step), step), :] = src[pl.ds(r, step), :].astype(F32)
            return 0

        lax.fori_loop(0, rows // step, body, 0)

    def columns(first, start, stride):
        return [big[pl.ds(first + s, dm, stride=stride), :].astype(BF16) for s in range(start, start + 2)]

    with jax.named_scope("relay_kv"):
        for ld in ld_k:
            ld.wait()
        unpack(wkr, 0, 2 * dm)
    ld_x.wait()
    with jax.named_scope("kvproj"):
        kp = jnp.dot(x2[h], jnp.concatenate(columns(0, 0, 2), axis=1), preferred_element_type=F32)
        for ld in ld_v:
            ld.wait()
        unpack(wvr, 2 * dm, 2 * dm)
        n_wq = wq_sem.shape[0]
        rows_wq = dm // n_wq
        head0 = pl.multiple_of(h * g, g)
        ld_q = [load(wq_hbm.at[pl.ds(i * rows_wq, rows_wq), pl.ds(head0, g), :], wqr.at[pl.ds(i * rows_wq, rows_wq)], wq_sem.at[i])
                for i in range(n_wq)]
        vp = jnp.dot(x2[h], jnp.concatenate(columns(2 * dm, 0, 2), axis=1), preferred_element_type=F32)
    ld_l.wait()
    ld_b.wait()
    t0 = pl.multiple_of(h * tok, tok)
    cb, sb = bas[0, pl.ds(c, 1), :], bas[1, pl.ds(c, 1), :]
    cl, sl = loc[0, pl.ds(t0, tok), :], loc[1, pl.ds(t0, tok), :]
    cos_k = cl * cb - sl * sb
    sin_k = sl * cb + cl * sb
    lane = lax.broadcasted_iota(jnp.int32, (tok, hd), 1)
    sin_k = jnp.where(lane < hd // 2, -sin_k, sin_k)
    for hh in range(2):
        k = kp[:, hh * hd:(hh + 1) * hd]
        k = (k * cos_k + pltpu.roll(k, hd // 2, 1) * sin_k).astype(BF16)
        v = vp[:, hh * hd:(hh + 1) * hd]
        own[hh, 0] = k
        own[hh, 1] = v.T.astype(BF16)
    kv[0, 0, h] = own[h, 0]
    kv[0, 1, h] = own[h, 1]

    with jax.named_scope("barrier"):
        pl.semaphore_wait(barrier, n_sent)
    x_copy = pltpu.make_async_remote_copy(src_ref=x2.at[h], dst_ref=x2.at[h], send_sem=xs_sem, recv_sem=xr_sem,
                                          device_id=dev(c, oh), device_id_type=MESH)

    p_copy = [pltpu.make_async_remote_copy(src_ref=own.at[oh, part], dst_ref=kv.at[0, part, h], send_sem=ps_sem.at[part], recv_sem=pr_sem.at[part],
                                           device_id=dev(c, oh), device_id_type=MESH) for part in range(2)]

    def each_direct(act, first, group):
        for i, (cond, slot, chip) in enumerate(group, first):
            @pl.when(cond)
            def _():
                for part in range(2):
                    for hh in range(2):
                        act(pltpu.make_async_remote_copy(src_ref=own.at[hh, part], dst_ref=kv.at[slot, part, h], send_sem=ks_sem.at[i, part, hh],
                                                         recv_sem=kr_sem.at[slot, part, h], device_id=dev(chip, hh), device_id_type=MESH))

    relays = relay_row + relay_far + relay_5 + relay_7

    def each_relay(act, group, part):
        for item in group:
            cond, src, dst, chip = item
            i = [r is item for r in relays].index(True)

            @pl.when(cond)
            def _():
                act(pltpu.make_async_remote_copy(src_ref=kv.at[src, part], dst_ref=kv.at[dst, part], send_sem=rs_sem.at[i, part],
                                                 recv_sem=rr_sem.at[dst, part], device_id=dev(chip, h), device_id_type=MESH))

    each_direct(lambda cp: cp.start(), 0, direct[:1])
    for cp in p_copy:
        cp.start()
    each_direct(lambda cp: cp.start(), 1, direct[1:])
    x_copy.start()

    ld_o = load(wo_hbm, wob, ld_sem.at[5])

    with jax.named_scope("relay_q"):
        dch = 128
        for i in range(n_wq):
            ld_q[i].wait()

            def unpack_q(t, _):
                d0 = pl.multiple_of(i * rows_wq + t * dch, dch)
                big[pl.ds(pl.multiple_of(d0 * g, dch * g), dch * g), :] = wqr[pl.ds(d0, dch)].astype(F32).reshape(dch * g, hd)
                return 0

            lax.fori_loop(0, rows_wq // dch, unpack_q, 0)
    each_direct(lambda cp: cp.start(), len(direct), later)
    half = hd // 2
    cl, sl = loc[0], loc[1]
    cs_t[0] = (cl * cb - sl * sb).T[:half]
    cs_t[1] = (sl * cb + cl * sb).T[:half]
    with jax.named_scope("xwait"):
        x_copy.wait_recv()
    xall = x2[...].reshape(2 * tok, dm)

    def proj_q(n):
        return jnp.dot(xall, jnp.concatenate(columns(0, 2 * n, g), axis=1), preferred_element_type=F32)

    with jax.named_scope("qproj"):
        for n in range(g // 2):
            qp = proj_q(n)
            for s in range(2):
                qt = qp[:, s * hd:(s + 1) * hd].T
                lo, hi = qt[:half], qt[half:]
                q_t[2 * n + s, :half] = (lo * cs_t[0] - hi * cs_t[1]).astype(BF16)
                q_t[2 * n + s, half:] = (hi * cs_t[0] + lo * cs_t[1]).astype(BF16)
    scale = hd ** -0.5 * math.log2(math.e)
    ki = lax.broadcasted_iota(jnp.int32, (2 * tok, 2 * tok), 0)
    qi = lax.broadcasted_iota(jnp.int32, (2 * tok, 2 * tok), 1)

    def attend(slot):
        kb = kv[slot, 0].reshape(2 * tok, hd)
        vb = jnp.concatenate([kv[slot, 1, 0], kv[slot, 1, 1]], axis=1)

        def weigh(n, s):
            if slot == 0:
                s = jnp.where(ki <= qi, s, -jnp.inf)
            if slot == last:
                s = jnp.where(ki > qi, s, -jnp.inf)
            top = jnp.max(s, axis=0, keepdims=True) * scale
            m_new = top if slot == 0 else jnp.maximum(m_s[n], top)
            p = jnp.exp2(s * scale - m_new)
            tot = jnp.sum(p, axis=0, keepdims=True)
            alpha = None
            if slot == 0:
                l_s[n] = tot
            else:
                alpha = jnp.exp2(m_s[n] - m_new)
                l_s[n] = l_s[n] * alpha + tot
            m_s[n] = m_new
            return p.astype(BF16), alpha

        def gather(n, p, alpha):
            r = jnp.dot(vb, p, preferred_element_type=F32)
            acc[n] = r if alpha is None else acc[n] * alpha + r

        scores, held = [], None
        for n in range(g):
            while len(scores) < min(n + 3, g):
                scores.append(jnp.dot(kb, q_t[len(scores)], preferred_element_type=F32))
            p, alpha = weigh(n, scores[n])
            if held is not None:
                gather(*held)
            held = (n, p, alpha)
        gather(*held)

    def landed(slot, relayed, group=(), parts=(0, 1)):
        for part in parts:
            with jax.named_scope(f"w{slot}{'kv'[part]}{'r' * relayed}"):
                if relayed:
                    pltpu.make_async_copy(kv.at[0, part], kv.at[slot, part], rr_sem.at[slot, part]).wait()
                else:
                    for s in range(2):
                        pltpu.make_async_copy(own.at[0, part], kv.at[slot, part, s], kr_sem.at[slot, part, s]).wait()
            each_relay(lambda cp: cp.start(), group, part)

    def visit(slot, here, relayed=False, got_if=None, group=()):
        @pl.when(here)
        def _():
            if got_if is None:
                landed(slot, relayed, group)
            elif got_if is edge:
                pl.when(edge)(lambda: landed(slot, True, group))
                pl.when(jnp.logical_not(edge))(lambda: landed(slot, False, group))
            elif got_if is not True:
                pl.when(jnp.logical_not(got_if))(lambda: landed(slot, relayed, group))
            with jax.named_scope(f"att{slot}"):
                attend(slot)

    pl.when(both(dn1, jnp.logical_not(edge)))(lambda: landed(4, False, relay_row, (0,)))
    with jax.named_scope("pwait"):
        for cp in p_copy:
            cp.wait_recv()
    with jax.named_scope("att0"):
        attend(0)
    pl.when(both(dn1, edge))(lambda: landed(4, False, relay_row, (0,)))
    pl.when(dn1)(lambda: landed(4, False, relay_row, (1,)))
    visit(4, dn1, got_if=True)
    visit(1, col >= 1)
    visit(8, dn2, got_if=edge, group=relay_far)

    @pl.when(both(dn1, col < 2))
    def _():
        for part in range(2):
            landed(5, True, relay_5, (part,))
            landed(7, True, relay_7, (part,))

    visit(2, col >= 2)
    visit(3, col >= 3)
    visit(5, dn1, relayed=True, got_if=col < 2)
    visit(7, dn1, relayed=True, got_if=col < 2)
    visit(3, both(dn2, col < 3), relayed=True)
    visit(6, dn1, relayed=True)
    visit(1, both(dn2, col < 1), relayed=True)
    visit(2, both(dn2, col < 2), relayed=True)

    def finish(n, _):
        o = (acc[n] / l_s[n]).T.astype(BF16)
        c0 = pl.multiple_of(n * hd, hd)
        o_send[0, :, pl.ds(c0, hd)] = o[:tok]
        o_send[1, :, pl.ds(c0, hd)] = o[tok:]
        return 0

    with jax.named_scope("finish"):
        lax.fori_loop(0, g, finish, 0, unroll=True)
    o_copy = pltpu.make_async_remote_copy(src_ref=o_send.at[oh], dst_ref=o_all, send_sem=os_sem, recv_sem=or_sem,
                                          device_id=dev(c, oh), device_id_type=MESH)
    o_copy.start()
    with jax.named_scope("wowait"):
        ld_o.wait()
    w0 = pl.multiple_of(h * g * hd, g * hd)
    w1 = pl.multiple_of(oh * g * hd, g * hd)
    o_own = o_send[h]
    n_y = 4
    cols = dm // n_y

    def own_part(i, _):
        c0 = pl.multiple_of(i * cols, cols)
        y_v[:, pl.ds(c0, cols)] = jnp.dot(o_own, wob[pl.ds(w0, g * hd), pl.ds(c0, cols)], preferred_element_type=F32)
        return 0

    with jax.named_scope("wo_own"):
        lax.fori_loop(0, n_y, own_part, 0, unroll=True)
    with jax.named_scope("owait"):
        o_copy.wait_recv()
    o_oth = o_all[...]
    with jax.named_scope("wo_oth"):
        for i in range(n_y):
            cs = slice(i * cols, (i + 1) * cols)
            y_ref[:, cs] = (y_v[:, cs] + jnp.dot(o_oth, wob[pl.ds(w1, g * hd), cs], preferred_element_type=F32)).astype(BF16)
    with jax.named_scope("sendwait"):
        x_copy.wait_send()
        for cp in p_copy:
            cp.wait_send()
        o_copy.wait_send()
        each_direct(lambda cp: cp.wait_send(), 0, direct + later)

        for part in range(2):
            each_relay(lambda cp: cp.wait_send(), relays, part)


def solution(mesh):
    n_outer, n_inner = mesh.shape['cpo'], mesh.shape['cpi']

    def local_fn(hidden, w_q, w_k, w_v, w_o):
        tok, dm = hidden.shape
        hq, hd = w_q.shape[1], w_q.shape[2]
        g = hq // 2
        nb = WINDOW // (2 * tok) + 1
        loc, bas = rope_tables(2 * tok, n_outer * n_inner // 2, hd)
        dims = (n_outer, n_inner, tok, dm, g, hd, nb)
        scratch = [
            pltpu.VMEM((2, tok, dm), BF16), pltpu.VMEM((dm, g, hd), BF16), pltpu.VMEM((2 * dm, hd), BF16), pltpu.VMEM((2 * dm, hd), BF16),
            pltpu.VMEM((dm * g, hd), F32), pltpu.VMEM((hq * hd, dm), BF16),
            pltpu.VMEM(loc.shape, F32), pltpu.VMEM(bas.shape, F32),
            pltpu.VMEM((2, 2, tok, hd), BF16), pltpu.VMEM((nb, 2, 2, tok, hd), BF16),
            pltpu.VMEM((g, hd, 2 * tok), BF16), pltpu.VMEM((2, hd // 2, 2 * tok), F32),
            pltpu.VMEM((g, 1, 2 * tok), F32), pltpu.VMEM((g, 1, 2 * tok), F32), pltpu.VMEM((g, hd, 2 * tok), F32),
            pltpu.VMEM((tok, g * hd), BF16), pltpu.VMEM((2, tok, g * hd), BF16), pltpu.VMEM((tok, dm), F32),
            pltpu.SemaphoreType.DMA((8,)), pltpu.SemaphoreType.DMA((4,)), pltpu.SemaphoreType.DMA, pltpu.SemaphoreType.DMA,
            pltpu.SemaphoreType.DMA((2,)), pltpu.SemaphoreType.DMA((2,)), pltpu.SemaphoreType.DMA((nb, 2, 2)), pltpu.SemaphoreType.DMA((nb, 2, 2)),
            pltpu.SemaphoreType.DMA((nb, 2)), pltpu.SemaphoreType.DMA((nb, 2)), pltpu.SemaphoreType.DMA, pltpu.SemaphoreType.DMA,
        ]
        return pl.pallas_call(
            functools.partial(kernel, dims),
            out_shape=pltpu.VMEM((tok, dm), BF16),
            in_specs=[pl.BlockSpec(memory_space=pl.ANY)] * 7,
            out_specs=pl.BlockSpec(memory_space=pltpu.VMEM),
            scratch_shapes=scratch,
            compiler_params=pltpu.CompilerParams(collective_id=0, has_side_effects=True, vmem_limit_bytes=56 * 1024 * 1024),
        )(hidden, w_q, w_k.reshape(2 * dm, hd), w_v.reshape(2 * dm, hd), w_o.reshape(hq * hd, dm), jnp.asarray(loc), jnp.asarray(bas))

    return jax.shard_map(local_fn, mesh=mesh,
                         in_specs=(P(('dp', 'cpo', 'cpi'), None), P(), P(), P(), P()),
                         out_specs=P(('dp', 'cpo', 'cpi'), None), check_vma=False)
```

time: 30.2 us -> 27.9 us (0.924)
  the two profiles are of different devices: /device:TPU:33 before, /device:TPU:97 now
where the time goes in v3:
time: 27.9 us; the launch traced here: 27.8 us
  Pallas kernels  27 us (97%)
  local copies, waits for them, and re-layouts  0.8 us (3%)
    pallas_call x1, Pallas kernels, local_fn(): pl.pallas_call(functools.partial(kernel, dims), out_shape=pltpu.VMEM((tok...  27 us
    unnamed x1, local copies, waits for them, and re-layouts  0.8 us

profile of v3, /device:TPU:97, one launch (start us, length us, event | category | flops | bytes accessed | tf_op | source)
XLA Modules:
  0.0 27.8 jit_solution(3916263561490544204)
XLA Ops:
  0.0 27.0 %shard_map.73 = bf16[128,2048]{1,0:T(8,128)(2,1)S(1)} custom-call(bf16[128,2048]{1,0:T(8,128)(2,1)} %x_hbm.1, bf16[2048,16,128]{2,1,0:T(8,128)(2,1)} %wq_hbm.1, bf16[4096,128]{1,0:T(8,128)(2,1)} %bitcast.4, bf16[4096,128]{1,0:T(8,128)(2,1)} %bitcast.5, bf16[2048,2048]{1,0:T(8,128)(2,1)} %bitcast.3, f32[2,256,128]{2,1,0:T(8,128)} %constant.4.clone.loc_hbm, ...), custom_call_target="tpu_custom_call" | custom-call | tf_op jit(solution)/shard_map/pallas_call | solution.py:364
  27.0 0.8 %copy.9 = bf16[128,2048]{1,0:T(8,128)(2,1)} copy(bf16[128,2048]{1,0:T(8,128)(2,1)S(1)} %shard_map.73) | data formatting | bytes 1048576
